TPU v7x, 128 devices: a whole 4x4x4 slice. The times are simulated.
128 devices in a mesh: aa: 16 (over x, z_hi, core), ba: 8 (over y, z_lo).
Axes of the slice: x: 4, y: 4, z: 4 (z_hi: 2, z_lo: 2; z = z_hi * 2 + z_lo), core: 2. Of those that a mesh axis runs over, the one named last changes fastest.
Arguments:
- amplitudes: bfloat16 [2048, 2048], P('aa', 'ba'), may hold values from -6 to 6
- code: int32 [32, 2048], replicated, may hold values from -2048 to 2048, as said below
- counts: int32 [128], replicated, may hold values from 1 to 16, as said below
- pair_irrep: int32 [32], replicated, may hold values from 0 to 7
- integrals: bfloat16 [32, 32], replicated, may hold values from -3 to 3
- one_body: bfloat16 [32], replicated, may hold values from -1.5 to 1.5
Outputs:
- sigma: bfloat16 [2048, 2048], P('aa', 'ba')
Inputs may be any that keep to these rules, and one draw needn't show every extreme that they name: |code| - 1 names the target string of a replacement and the sign of code its sign; some entries reach both ends. `counts`: the live strings of fine block j fill its first slots, from slot j * 16 on; in every draw some block is full and some holds one string.
All inputs are finite; a program needn't handle non-finite values.
Results may differ from a plain program's by a relative error of at most 0.0045.
Values may be sent and summed in bfloat16 or wider, within the bound.
A program may use at most 128 MiB of HBM per device.

v0:
```python
import jax
import jax.numpy as jnp
from jax import lax
from jax.sharding import PartitionSpec as P


def one_hot(tables, signs, first, width):
    ids = first + jnp.arange(width, dtype=jnp.int32)
    return jnp.where(
        tables[:, :, None] == ids[None, None, :], signs[:, :, None], jnp.zeros((), jnp.bfloat16)
    )


def alpha_term(tables, signs, values, start_a, rows_a, rows_b, count):
    groups = tables.shape[0] // 8
    rows_t = tables.reshape(groups, 8, count)
    rows_s = signs.reshape(groups, 8, count)

    def one_group(carry, items):
        tab, sgn, val = items
        hot = one_hot(tab, sgn, start_a, rows_a)
        return (
            carry + jnp.einsum("prk,pkb->rb", hot, val, preferred_element_type=jnp.float32),
            None,
        )

    total, _ = lax.scan(
        one_group,
        jnp.zeros((count, rows_b), jnp.float32),
        (rows_t, rows_s, values.reshape(groups, 8, rows_a, rows_b)),
    )
    return total


def per_device(amplitudes, code, counts, pair_irrep, integrals, one_body):
    rows_a, rows_b = amplitudes.shape
    pairs, strings = code.shape
    groups = pairs // 8
    capacity = strings // counts.shape[0]
    slots = jnp.arange(strings, dtype=jnp.int32)
    live_all = (slots % capacity < jnp.repeat(counts, capacity)).astype(jnp.bfloat16)
    start_a = lax.axis_index("aa") * rows_a
    start_b = lax.axis_index("ba") * rows_b
    live_a = lax.dynamic_slice_in_dim(live_all, start_a, rows_a)
    live_b = lax.dynamic_slice_in_dim(live_all, start_b, rows_b)
    masked = amplitudes * (live_a[:, None] * live_b[None, :])
    target = jnp.abs(code) - 1
    signs = jnp.sign(code).astype(jnp.bfloat16)
    target_a = lax.dynamic_slice_in_dim(target, start_a, rows_a, 1).reshape(groups, 8, rows_a)
    signs_a = lax.dynamic_slice_in_dim(signs, start_a, rows_a, 1).reshape(groups, 8, rows_a)
    target_b = lax.dynamic_slice_in_dim(target, start_b, rows_b, 1).reshape(groups, 8, rows_b)
    signs_b = lax.dynamic_slice_in_dim(signs, start_b, rows_b, 1).reshape(groups, 8, rows_b)
    piece = lax.all_gather(masked, "ba", axis=1, tiled=True)
    start = jnp.int32(0)

    def one_group(items):
        tab, sgn = items
        hot = one_hot(tab, sgn, start, piece.shape[1])
        return jnp.einsum("pkc,ic->pik", hot, piece, preferred_element_type=jnp.float32)

    beta_sum = lax.map(one_group, (target_b, signs_b)).reshape(pairs, rows_a, rows_b)
    dbeta = (beta_sum * live_b[None, None, :]).astype(jnp.bfloat16)
    alpha_piece = lax.all_gather(masked, "aa", axis=0, tiled=True)
    alpha_start = jnp.int32(0)

    def one_group(items):
        tab, sgn = items
        hot = one_hot(tab, sgn, alpha_start, alpha_piece.shape[0])
        return jnp.einsum("pkj,jb->pkb", hot, alpha_piece, preferred_element_type=jnp.float32)

    alpha_sum = lax.map(one_group, (target_a, signs_a)).reshape(pairs, rows_a, rows_b)
    dalpha = (alpha_sum * live_a[None, :, None]).astype(jnp.bfloat16)
    weights = jnp.where(
        pair_irrep[:, None] == pair_irrep[None, :], integrals, jnp.zeros((), jnp.bfloat16)
    )
    gbeta_full = jnp.einsum("pq,qik->pik", weights, dbeta, preferred_element_type=jnp.float32)
    galpha_full = jnp.einsum("pq,qik->pik", weights, dalpha, preferred_element_type=jnp.float32)
    gbeta = gbeta_full.astype(jnp.bfloat16)
    combined = (gbeta_full + 0.5 * galpha_full).astype(jnp.bfloat16)
    local = jnp.einsum("p,pik->ik", one_body, dbeta, preferred_element_type=jnp.float32)
    local = local + jnp.einsum("p,pik->ik", one_body, dalpha, preferred_element_type=jnp.float32)
    half_beta = gbeta * 0.5
    gathered_piece = lax.all_gather(half_beta, "ba", axis=2, tiled=True)
    gathered_start = jnp.int32(0)
    width = gathered_piece.shape[2]

    def one_group(acc, items):
        tab, sgn, val = items
        hot = one_hot(tab, sgn, gathered_start, width)
        return (acc + jnp.einsum("pbk,pak->ab", hot, val, preferred_element_type=jnp.float32), None)

    total, _ = lax.scan(
        one_group,
        jnp.zeros((rows_a, rows_b), jnp.float32),
        (target_b, signs_b, gathered_piece.reshape(groups, 8, rows_a, width)),
    )
    beta_part = total
    alpha_rows = lax.psum_scatter(
        alpha_term(target, signs, combined, start_a, rows_a, rows_b, lax.axis_size("aa") * rows_a),
        "aa",
        scatter_dimension=0,
        tiled=True,
    )
    total = local + beta_part + alpha_rows
    return (total * (live_a[:, None] * live_b[None, :])).astype(jnp.bfloat16)


def solution(mesh):
    placed = (P("aa", "ba"), P(), P(), P(), P(), P())
    return jax.shard_map(
        per_device, mesh=mesh, in_specs=placed, out_specs=P("aa", "ba"), check_vma=False
    )
```

profile of v0, /device:TPU:1, one launch (start us, length us, event | category | flops | bytes accessed | tf_op | source)
XLA Modules:
  0.0 476.8 jit_solution(13989300065784865499)
XLA Ops:
  9.2 25.1 %all_gather.9 = bf16[128,2048]{1,0:T(8,128)(2,1)S(1)} all-gather(bf16[128,256]{1,0:T(8,128)(2,1)} %multiply_multiply_fusion), channel_id=1, replica_groups=mesh['aa'=16,'ba'=8] {'ba'}, dimensions={1}, use_global_device_ids=true | all-gather | bytes 589824 | tf_op jit(solution)/shard_map/all_gather | solution.py:53
  35.4 13.7 %while.42 = (s32[]{:T(128)}, f32[4,8,128,256]{2,3,1,0:T(8,128)}, s32[4,8,256]{2,1,0:T(8,128)S(1)}, bf16[4,8,256]{2,1,0:T(8,128)(2,1)S(1)}, bf16[128,2048]{1,0:T(8,128)(2,1)S(1)}, /*index=5*/s32[]{:T(128)}) while((s32[]{:T(128)}, f32[4,8,128,256]{2,3,1,0:T(8,128)}, s32[4,8,256]{2,1,0:T(8,128)S(1)}, bf16[4,8,256]{2,1,0:T(8,128)(2,1)S(1)}, ...), condition=%wide.region_1.2_spmd, body=%wide.region_0.1_spmd.sunk | while | flops 1082130432 | bytes 1609817 | solution.py:61
  35.4 3.4 fusion.91
  38.8 3.4 fusion.91
  42.3 3.4 fusion.91
  45.7 3.4 fusion.91
  49.1 5.5 %copy.13 = f32[32,128,256]{2,0,1:T(8,128)} copy(f32[32,128,256]{1,2,0:T(8,128)} %bitcast.130) | data formatting | bytes 8388608 | tf_op jit(solution)/shard_map/reshape | solution.py:61
  54.6 5.5 %convert_multiply_fusion = (bf16[32,128,256]{2,0,1:T(8,128)(2,1)}, f32[32,128,256]{2,0,1:T(8,128)}) fusion(f32[32,128,256]{2,0,1:T(8,128)} %copy.13, f32[256]{0:T(256)S(1)} %get-tuple-element.237, bf16[32,32]{1,0:T(8,128)(2,1)S(1)} %copy-done.2, s32[32]{0:T(128)S(1)} %copy-done.3), kind=kOutput, calls=%fused_computation.55 | convolution fusion | flops 71305216 | bytes 10488960 | tf_op jit(solution)/shard_map/pq,qik->pik/dot_general | solution.py:76
  60.3 2.6 fusion.52
  63.0 14.2 %while.43 = (s32[]{:T(128)}, f32[4,8,128,256]{3,2,1,0:T(8,128)}, s32[4,8,128]{2,1,0:T(8,128)S(1)}, bf16[4,8,128]{2,1,0:T(8,128)(2,1)S(1)}, bf16[2048,256]{1,0:T(8,128)(2,1)}, /*index=5*/s32[]{:T(128)}) while((s32[]{:T(128)}, f32[4,8,128,256]{3,2,1,0:T(8,128)}, s32[4,8,128]{2,1,0:T(8,128)S(1)}, bf16[4,8,128]{2,1,0:T(8,128)(2,1)S(1)}, ...), condition=%wide.region_3.4_spmd, body=%wide.region_2.3_spmd.sunk | while | flops 1077936128 | bytes 2115673 | solution.py:71
  63.0 3.6 fusion.94
  66.6 3.5 fusion.94
  70.1 3.5 fusion.94
  73.6 3.5 fusion.94
  77.1 4.8 %fusion.65 = f32[1,128,256]{2,0,1:T(1,128)S(1)} fusion(bf16[32]{0:T(256)(128)(2,1)S(1)} %copy-done, f32[32,128,256]{2,1,0:T(8,128)} %bitcast.128, f32[128]{0:T(128)S(1)} %get-tuple-element.235), kind=kOutput, calls=%fused_computation.80 | convolution fusion | flops 4194304 | bytes 4325952 | tf_op jit(solution)/shard_map/p,pik->ik/dot_general | solution.py:81
  81.9 5.0 %fusion.50 = bf16[4,8,128,256]{3,1,0,2:T(8,128)(2,1)S(1)} fusion(f32[32,128,256]{2,0,1:T(8,128)S(1)} %copy-done.1, bf16[32,32]{1,0:T(8,128)(2,1)S(1)} %copy-done.2, s32[32]{0:T(128)S(1)} %copy-done.3, f32[32,128,256]{2,1,0:T(8,128)} %bitcast.129, f32[128]{0:T(128)S(1)} %get-tuple-element.235), kind=kOutput, calls=%fused_computation.56 | convolution fusion | flops 72353792 | bytes 10488448 | tf_op jit(solution)/shard_map/pq,qik->pik/dot_general | solution.py:77
  86.9 27.8 %while.45 = (s32[]{:T(128)}, f32[2048,256]{1,0:T(8,128)}, s32[4,8,2048]{2,1,0:T(8,128)S(1)}, s32[]{:T(128)}, bf16[4,8,2048]{2,1,0:T(8,128)(2,1)S(1)}, /*index=5*...) while((s32[]{:T(128)}, f32[2048,256]{1,0:T(8,128)}, s32[4,8,2048]{2,1,0:T(8,128)S(1)}, ...), condition=%wide.region_7.8_spmd.clone, body=%wide.region_6.7_spmd.clone.sunk | while | flops 1078984832 | bytes 6063223 | solution.py:27
  87.1 6.1 %fusion.98 = f32[2048,256]{1,0:T(8,128)} fusion(s32[128]{0:T(128)S(1)} %iota_add_fusion.2, s32[8,2048]{1,0:T(8,128)S(1)} %dynamic-slice_bitcast_fusion.26, f32[2048,256]{1,0:T(8,128)} %get-tuple-element.419, bf16[8,2048]{1,0:T(8,128)(2,1)S(1)} %dynamic-slice_bitcast_fusion.27, pred[]{:T(512)S(6)} %compare.8, ...), kind=kOutput, calls=%fused_computation.42.clone.1 | convolution fusion | flops 1078984704 | bytes 4817409 | tf_op jit(solution)/shard_map/while/body/eval_jaxpr/prk,pkb->rb/dot_general | solution.py:23
  93.2 7.1 %fusion.98 = f32[2048,256]{1,0:T(8,128)} fusion(s32[128]{0:T(128)S(1)} %iota_add_fusion.2, s32[8,2048]{1,0:T(8,128)S(1)} %dynamic-slice_bitcast_fusion.26, f32[2048,256]{1,0:T(8,128)} %get-tuple-element.419, bf16[8,2048]{1,0:T(8,128)(2,1)S(1)} %dynamic-slice_bitcast_fusion.27, pred[]{:T(512)S(6)} %compare.8, ...), kind=kOutput, calls=%fused_computation.42.clone.1 | convolution fusion | flops 1078984704 | bytes 4817409 | tf_op jit(solution)/shard_map/while/body/eval_jaxpr/prk,pkb->rb/dot_general | solution.py:23
  100.4 7.1 %fusion.98 = f32[2048,256]{1,0:T(8,128)} fusion(s32[128]{0:T(128)S(1)} %iota_add_fusion.2, s32[8,2048]{1,0:T(8,128)S(1)} %dynamic-slice_bitcast_fusion.26, f32[2048,256]{1,0:T(8,128)} %get-tuple-element.419, bf16[8,2048]{1,0:T(8,128)(2,1)S(1)} %dynamic-slice_bitcast_fusion.27, pred[]{:T(512)S(6)} %compare.8, ...), kind=kOutput, calls=%fused_computation.42.clone.1 | convolution fusion | flops 1078984704 | bytes 4817409 | tf_op jit(solution)/shard_map/while/body/eval_jaxpr/prk,pkb->rb/dot_general | solution.py:23
  107.6 7.1 %fusion.98 = f32[2048,256]{1,0:T(8,128)} fusion(s32[128]{0:T(128)S(1)} %iota_add_fusion.2, s32[8,2048]{1,0:T(8,128)S(1)} %dynamic-slice_bitcast_fusion.26, f32[2048,256]{1,0:T(8,128)} %get-tuple-element.419, bf16[8,2048]{1,0:T(8,128)(2,1)S(1)} %dynamic-slice_bitcast_fusion.27, pred[]{:T(512)S(6)} %compare.8, ...), kind=kOutput, calls=%fused_computation.42.clone.1 | convolution fusion | flops 1078984704 | bytes 4817409 | tf_op jit(solution)/shard_map/while/body/eval_jaxpr/prk,pkb->rb/dot_general | solution.py:23
  114.7 278.1 %all-gather.5.cloned.1.call-done = bf16[32,128,2048]{2,0,1:T(8,128)(2,1)} async-done(((bf16[32,128,256]{2,0,1:T(8,128)(2,1)}), bf16[32,128,2048]{2,0,1:T(8,128)(2,1)}) %all-gather.5.cloned.1.call-update) | async-done | bytes 16777232 | tf_op jit(solution)/shard_map/all_gather | solution.py:83
  392.8 40.3 %while.44 = (s32[]{:T(128)}, f32[128,256]{1,0:T(8,128)S(1)}, bf16[4,8,128,2048]{3,1,0,2:T(8,128)(2,1)}, s32[4,8,256]{2,1,0:T(8,128)S(1)}, bf16[4,8,256]{2,1,0:T(8,128)(2,1)S(1)}, /*index=5*/s32[]{:T(128)}, s32[]{:T(128)}) while((s32[]{:T(128)}, f32[128,256]{1,0:T(8,128)S(1)}, bf16[4,8,128,2048]{3,1,0,2:T(8,128)(2,1)}, ...), condition=%wide.region_5.6_spmd.clone, body=%wide.region_4.5_spmd.clone.sunk | while | flops 1082195968 | bytes 29659240 | solution.py:92
  392.8 2.5 constant_dynamic-slice_fusion.4
  397.2 5.5 %fusion.97 = f32[128,256]{1,0:T(8,128)S(1)} fusion(bf16[1,8,128,2048]{3,1,0,2:T(8,128)(2,1)S(1)} %constant_dynamic-slice_fusion.4, f32[128,256]{1,0:T(8,128)S(1)} %get-tuple-element.442, pred[]{:T(512)S(6)} %compare.7, bf16[8,256,2048]{2,1,0:T(8,128)(2,1)S(1)} %fusion.96), kind=kOutput, calls=%fused_computation.32.clone.2 | convolution fusion | flops 1073807360 | bytes 12845057 | tf_op jit(solution)/shard_map/while/body/eval_jaxpr/pbk,pak->ab/dot_general | solution.py:90
  402.8 2.5 constant_dynamic-slice_fusion.4
  407.3 5.5 %fusion.97 = f32[128,256]{1,0:T(8,128)S(1)} fusion(bf16[1,8,128,2048]{3,1,0,2:T(8,128)(2,1)S(1)} %constant_dynamic-slice_fusion.4, f32[128,256]{1,0:T(8,128)S(1)} %get-tuple-element.442, pred[]{:T(512)S(6)} %compare.7, bf16[8,256,2048]{2,1,0:T(8,128)(2,1)S(1)} %fusion.96), kind=kOutput, calls=%fused_computation.32.clone.2 | convolution fusion | flops 1073807360 | bytes 12845057 | tf_op jit(solution)/shard_map/while/body/eval_jaxpr/pbk,pak->ab/dot_general | solution.py:90
  412.9 2.6 constant_dynamic-slice_fusion.4
  417.5 5.5 %fusion.97 = f32[128,256]{1,0:T(8,128)S(1)} fusion(bf16[1,8,128,2048]{3,1,0,2:T(8,128)(2,1)S(1)} %constant_dynamic-slice_fusion.4, f32[128,256]{1,0:T(8,128)S(1)} %get-tuple-element.442, pred[]{:T(512)S(6)} %compare.7, bf16[8,256,2048]{2,1,0:T(8,128)(2,1)S(1)} %fusion.96), kind=kOutput, calls=%fused_computation.32.clone.2 | convolution fusion | flops 1073807360 | bytes 12845057 | tf_op jit(solution)/shard_map/while/body/eval_jaxpr/pbk,pak->ab/dot_general | solution.py:90
  423.1 2.5 constant_dynamic-slice_fusion.4
  427.6 5.5 %fusion.97 = f32[128,256]{1,0:T(8,128)S(1)} fusion(bf16[1,8,128,2048]{3,1,0,2:T(8,128)(2,1)S(1)} %constant_dynamic-slice_fusion.4, f32[128,256]{1,0:T(8,128)S(1)} %get-tuple-element.442, pred[]{:T(512)S(6)} %compare.7, bf16[8,256,2048]{2,1,0:T(8,128)(2,1)S(1)} %fusion.96), kind=kOutput, calls=%fused_computation.32.clone.2 | convolution fusion | flops 1073807360 | bytes 12845057 | tf_op jit(solution)/shard_map/while/body/eval_jaxpr/pbk,pak->ab/dot_general | solution.py:90
  433.1 35.6 %reduce-scatter.2.cloned.1.call-done = f32[128,256]{1,0:T(8,128)} async-done(((f32[2048,256]{1,0:T(8,128)}), f32[128,256]{1,0:T(8,128)}) %reduce-scatter.2.cloned.1.call-update) | async-done | bytes 131088 | tf_op jit(solution)/shard_map/reduce_scatter | solution.py:98
  (75 shorter events, 13.9 us)
Async XLA Ops:
  6.5 53.8 %copy-start = (bf16[32]{0:T(256)(128)(2,1)S(1)}, bf16[32]{0:T(256)(128)(2,1)}, u32[]{:S(2)}) copy-start(bf16[32]{0:T(256)(128)(2,1)} %param.19) | copy-start | bytes 196
  6.5 56.4 %all-gather.3.cloned.1.call-start = ((), (), s32[]{:S(2)}) async-start(), calls=%async_computation.1 | async-start | bytes 1114112 | tf_op jit(solution)/shard_map/all_gather | solution.py:63
  9.1 383.6 %all-gather.5.cloned.1.call-start = ((), (), s32[]{:S(2)}) async-start(), calls=%async_computation.2 | async-start | bytes 18874368 | tf_op jit(solution)/shard_map/all_gather | solution.py:83
  49.1 5.5 %copy-start.2 = (bf16[32,32]{1,0:T(8,128)(2,1)S(1)}, bf16[32,32]{1,0:T(8,128)(2,1)}, u32[]{:S(2)}) copy-start(bf16[32,32]{1,0:T(8,128)(2,1)} %param.18) | copy-start | bytes 6148
  49.1 5.5 %copy-start.3 = (s32[32]{0:T(128)S(1)}, s32[32]{0:T(128)}, u32[]{:S(2)}) copy-start(s32[32]{0:T(128)} %param.17) | copy-start | bytes 388
  60.2 408.5 %reduce-scatter.2.cloned.1.call-start = ((), (), s32[]{:S(2)}) async-start(), calls=%async_computation.3 | async-start | bytes 2228224 | tf_op jit(solution)/shard_map/reduce_scatter | solution.py:98
  77.1 4.8 %copy-start.1 = (f32[32,128,256]{2,0,1:T(8,128)S(1)}, f32[32,128,256]{2,0,1:T(8,128)}, u32[]{:S(2)}) copy-start(f32[32,128,256]{2,0,1:T(8,128)} %get-tuple-element.243) | copy-start | bytes 12582916
Sparse Core Ops, SparseCore 0:
  9.7 48.6 all-gather.2
  60.3 332.3 all-gather.4
  396.7 71.9 reduce-scatter.1
where the time goes:
time: 479 us; the launch traced here: 477 us
  waiting for transfers between devices  314 us (66%)
  matrix products  95 us (20%)
  blocking collectives  25.1 us (5%)
  local copies, waits for them, and re-layouts  17 us (4%)
  between operations  13.2 us (3%)
  other arithmetic  12.3 us (3%)
    all_gather x1, waiting for transfers between devices, per_device(): gathered_piece = lax.all_gather(half_beta, 'ba', axis=2, tiled=True)  278 us
    reduce_scatter x1, waiting for transfers between devices, per_device(): lax.psum_scatter(alpha_term(target, signs, combined, start_a, rows_a, row...  35.6 us
    dot_general x4, matrix products, one_group(): jnp.einsum('prk,pkb->rb', hot, val, preferred_element_type=jnp.float32)  27.2 us
    all_gather x1, blocking collectives, per_device(): piece = lax.all_gather(masked, 'ba', axis=1, tiled=True)  25.1 us
    dot_general x4, matrix products, one_group(): jnp.einsum('pbk,pak->ab', hot, val, preferred_element_type=jnp.float32)  22 us
    dot_general x4, matrix products, one_group(): jnp.einsum('pkj,jb->pkb', hot, alpha_piece, preferred_element_type=jnp.fl...  14.1 us
    dot_general x4, matrix products, one_group(): jnp.einsum('pkc,ic->pik', hot, piece, preferred_element_type=jnp.float32)  13.7 us
    dynamic_slice x4, local copies, waits for them, and re-layouts, per_device(): lax.scan(one_group, jnp.zeros((rows_a, rows_b), jnp.float32), (target_b,...  10.1 us
  transfers between devices with their start and end apart: 3, of which 2 were waited for; matrix products, arithmetic and copies ran while one was open for 25% of the time, Pallas kernels for 0%

commit v1 on v0

v1 whole, which is shorter than its diff:
```python
import functools

import jax
import jax.numpy as jnp
from jax import lax
from jax.experimental import pallas as pl
from jax.experimental.pallas import tpu as pltpu
from jax.sharding import PartitionSpec as P

F32 = jnp.float32
BF16 = jnp.bfloat16
MESH = pl.DeviceIdType.MESH


def iota(shape, axis):
    return lax.broadcasted_iota(jnp.int32, shape, axis)


def dot(a, b):
    return jnp.dot(a, b, preferred_element_type=F32)


def dot_nt(a, b):
    return lax.dot_general(a, b, (((1,), (1,)), ((), ())), preferred_element_type=F32)


def kernel(
    na, nb, capacity,
    amp_ref, code_ref, counts_ref, irrep_ref, integrals_ref, one_body_ref,
    out_ref,
    hi_ref, lo_ref, sg_ref, m2_ref, mt_ref, y_ref, z_ref, zt_ref, kron_ref, res_ref,
    mg_ref, tb_ref, ta_ref, rs_ref, rr_ref,
    m_send, m_recv, t_send, t_recv, c_send, c_recv, r_send, r_recv,
):
    ra, rb = amp_ref.shape
    pairs, ns = code_ref.shape
    his = ns // 128
    half = his // 2
    tr = ns // (na * nb)
    keys = his * tr
    ma = lax.axis_index("aa")
    mb = lax.axis_index("ba")

    def peer_a(k):
        return lax.rem(ma + k, na)

    def peer_b(k):
        return lax.rem(mb + k, nb)

    barrier = pltpu.get_barrier_semaphore()
    for k in range(1, na):
        pl.semaphore_signal(barrier, inc=1, device_id=(peer_a(k), mb), device_id_type=MESH)
    for k in range(1, nb):
        pl.semaphore_signal(barrier, inc=1, device_id=(ma, peer_b(k)), device_id_type=MESH)
    pl.semaphore_wait(barrier, na + nb - 2)

    def m_copy(k):
        return pltpu.make_async_remote_copy(
            src_ref=amp_ref, dst_ref=mg_ref.at[mb], send_sem=m_send.at[k], recv_sem=m_recv.at[mb],
            device_id=(ma, peer_b(k)), device_id_type=MESH)

    def m_arrived(k):
        src = peer_b(k)
        return pltpu.make_async_remote_copy(
            src_ref=amp_ref, dst_ref=mg_ref.at[src], send_sem=m_send.at[k], recv_sem=m_recv.at[src],
            device_id=(ma, src), device_id_type=MESH)

    for k in range(1, nb):
        m_copy(k).start()

    code = code_ref[...]
    target = jnp.abs(code) - 1
    hi = lax.shift_right_arithmetic(target, 7)
    lo = target & 127
    sg = jnp.where(code > 0, 1.0, jnp.where(code < 0, -1.0, 0.0)).astype(F32)
    hi_ref[...] = hi.astype(F32)
    lo_ref[...] = lo.astype(F32)
    sg_ref[...] = sg

    blocks = counts_ref.shape[1]
    counts = jnp.broadcast_to(counts_ref[...].astype(F32), (8, blocks)).astype(BF16)
    spread = (iota((blocks, ns), 1) // capacity == iota((blocks, ns), 0)).astype(F32).astype(BF16)
    slots = (iota((8, ns), 1) % capacity).astype(F32)
    live8 = jnp.where(slots < dot(counts, spread), 1.0, 0.0)
    live = live8[0:1]

    irr = jnp.broadcast_to(irrep_ref[...], (pairs, pairs))
    eye = iota((pairs, pairs), 0) == iota((pairs, pairs), 1)
    irr_col = jnp.sum(jnp.where(eye, irr, 0), axis=1, keepdims=True)
    w = jnp.where(irr_col == irr, integrals_ref[...].astype(F32), 0.0).astype(BF16)
    w_t = dot_nt(eye.astype(F32).astype(BF16), w).astype(BF16)

    grow = (iota((pairs * 8, pairs), 0) // 8 == iota((pairs * 8, pairs), 1)).astype(F32).astype(BF16)
    wide = dot_nt(dot(grow, w).astype(BF16), grow)
    same = iota((pairs * 8, pairs * 8), 0) % 8 == iota((pairs * 8, pairs * 8), 1) % 8
    kron_ref[...] = jnp.where(same, wide, 0.0).astype(BF16)

    first = mb * rb + ma * tr
    base = pl.multiple_of((first // 128) * 128, 128)
    off = first - base
    n = pairs * tr
    own = jnp.concatenate(
        [hi_ref[:, pl.ds(base, 128)], lo_ref[:, pl.ds(base, 128)], sg_ref[:, pl.ds(base, 128)]], axis=0
    ).astype(BF16)
    pick = (iota((128, n), 0) == off + iota((128, n), 1) % tr).astype(F32).astype(BF16)
    mine = dot(own, pick)
    here = iota((pairs, n), 0) == iota((pairs, n), 1) // tr
    k_hi = jnp.sum(jnp.where(here, mine[0:pairs], 0.0), axis=0, keepdims=True)
    k_lo = jnp.sum(jnp.where(here, mine[pairs : 2 * pairs], 0.0), axis=0, keepdims=True)
    k_sg = jnp.sum(jnp.where(here, mine[2 * pairs :], 0.0), axis=0, keepdims=True)
    here_b = here.astype(F32).astype(BF16)
    w_wide = dot(w_t, here_b)
    o_wide = dot(jnp.broadcast_to(one_body_ref[...], (8, pairs)), here_b)[0:1]
    k_lo_b = k_lo.astype(BF16)
    iota128 = iota((128, n), 0).astype(F32).astype(BF16)
    one = jnp.ones((), BF16)
    zero = jnp.zeros((), BF16)
    planes = jnp.concatenate([hi_ref[...], lo_ref[...], sg_ref[...] * live], axis=0).astype(BF16)
    got = jnp.zeros((3 * pairs, n), F32)
    for h in range(0, his, 2):
        sel = []
        for e in range(2):
            loc = jnp.where(k_hi == float(h + e), k_lo, -1.0).astype(BF16)
            sel.append(jnp.where(iota128 == loc, one, zero))
        got = got + dot(planes[:, h * 128 : (h + 2) * 128], jnp.concatenate(sel, axis=0))
    row = (iota((pairs, n), 1) % tr).astype(F32)
    key_all = got[0:pairs] * float(tr) + row
    lo_all = got[pairs : 2 * pairs]
    val_all = 0.5 * w_wide * got[2 * pairs :] * k_sg
    iota_keys = iota((keys, n), 0).astype(F32).astype(BF16)

    def histogram(key, low, val):
        a = jnp.where(iota_keys == key.astype(BF16), val.astype(BF16), zero)
        b = jnp.where(iota128 == low.astype(BF16), one, zero)
        return dot_nt(a, b)

    t_acc = histogram(k_hi * float(tr) + row[0:1], k_lo, o_wide * k_sg)
    for q in range(pairs):
        t_acc = t_acc + histogram(key_all[q : q + 1], lo_all[q : q + 1], val_all[q : q + 1])
    tb_ref[ma] = t_acc.astype(BF16).reshape(his, tr, 128)

    def t_copy(k, slot):
        return pltpu.make_async_remote_copy(
            src_ref=tb_ref.at[slot], dst_ref=tb_ref.at[slot], send_sem=t_send.at[k], recv_sem=t_recv.at[slot],
            device_id=(peer_a(k), mb), device_id_type=MESH)

    for k in range(1, na):
        t_copy(k, ma).start()

    low_a = ma * ra
    block_of = (iota((ra, blocks), 0) + low_a) // capacity
    count_a = jnp.sum(
        jnp.where(block_of == iota((ra, blocks), 1), counts_ref[...].astype(F32), 0.0), axis=1, keepdims=True)
    live_a = jnp.where(((iota((ra, 1), 0) + low_a) % capacity).astype(F32) < count_a, 1.0, 0.0)
    mg_ref[mb] = amp_ref[...]
    for k in range(1, nb):
        m_arrived(k).wait_recv()
    for j in range(nb):
        part = mg_ref[j].astype(F32) * live_a * live[:, j * rb : (j + 1) * rb]
        h = (j * rb) // (half * 128)
        at = j * rb - h * half * 128
        m2_ref[h * ra : (h + 1) * ra, at : at + rb] = part.astype(BF16)
    low_b = pl.multiple_of(mb * rb, 128)
    res_ref[...] = live8
    live_b = res_ref[0:1, pl.ds(low_b, rb)]
    mine_f = amp_ref[...].astype(F32) * live_a * live_b
    mt_ref[...] = mine_f.T.astype(BF16)

    iota_b = iota((128, rb), 0).astype(F32).astype(BF16)

    def gather(q, carry):
        hi_q = hi_ref[pl.ds(q, 1), pl.ds(low_b, rb)]
        lo_q = lo_ref[pl.ds(q, 1), pl.ds(low_b, rb)]
        sg_q = sg_ref[pl.ds(q, 1), pl.ds(low_b, rb)]
        upper = hi_q >= float(half)
        hi_in = jnp.where(upper, hi_q - float(half), hi_q)
        hots = []
        for j in range(half):
            loc = jnp.where(hi_in == float(j), lo_q, -1.0).astype(BF16)
            hots.append(jnp.where(iota_b == loc, one, zero))
        got_q = dot(m2_ref[...], jnp.concatenate(hots, axis=0))
        picked = jnp.where(jnp.broadcast_to(upper, (ra, rb)), got_q[ra:], got_q[:ra])
        y_ref[q] = picked * (sg_q * live_b)
        return carry

    lax.fori_loop(0, pairs, gather, 0)

    def mix(g, carry):
        at = pl.multiple_of(g * 8, 8)
        rows = y_ref[:, pl.ds(at, 8), :].reshape(pairs * 8, rb).astype(BF16)
        z_ref[:, pl.ds(at, 8), :] = dot(kron_ref[...], rows).reshape(pairs, 8, rb)
        return carry

    lax.fori_loop(0, ra // 8, mix, 0)

    def flip(p, carry):
        zt_ref[p] = z_ref[p].T.astype(BF16)
        return carry

    lax.fori_loop(0, pairs, flip, 0)

    for k in range(1, na):
        t_copy(k, peer_a(k)).wait_recv()
    ta_ref[mb] = tb_ref[:, ma]

    def c_copy(k):
        return pltpu.make_async_remote_copy(
            src_ref=tb_ref.at[:, ma], dst_ref=ta_ref.at[mb], send_sem=c_send.at[k], recv_sem=c_recv.at[mb],
            device_id=(ma, peer_b(k)), device_id_type=MESH)

    def c_arrived(k):
        src = peer_b(k)
        return pltpu.make_async_remote_copy(
            src_ref=tb_ref.at[:, ma], dst_ref=ta_ref.at[src], send_sem=c_send.at[k], recv_sem=c_recv.at[src],
            device_id=(ma, src), device_id_type=MESH)

    for k in range(1, nb):
        c_copy(k).start()

    res = jnp.zeros((rb, ra), F32)
    for h in range(0, his, 2):
        lhs = jnp.concatenate([tb_ref[:, h].reshape(rb, 128), tb_ref[:, h + 1].reshape(rb, 128)], axis=1)
        part = h // half
        at = (h - part * half) * 128
        res = res + dot_nt(lhs, m2_ref[part * ra : (part + 1) * ra, at : at + 256])
    total_ref = z_ref.at[0]
    total_ref[:, :] = res.T

    for k in range(1, nb):
        c_arrived(k).wait_recv()

    width = 2 * ra
    steps = na // 2
    group = min(pairs, 8)
    rows_t = width // (na * tr) if width >= na * tr else 0

    def r_copy(dest):
        return pltpu.make_async_remote_copy(
            src_ref=rs_ref.at[dest], dst_ref=rr_ref.at[ma], send_sem=r_send.at[dest], recv_sem=r_recv.at[ma],
            device_id=(dest, mb), device_id_type=MESH)

    def scatter(i, carry):
        d = lax.rem(ma // 2 + 1 + i, steps)
        at = pl.multiple_of(d * width, 128)
        acc = dot_nt(mt_ref[...], ta_ref[d].reshape(width, 128))
        for p0 in range(0, pairs, group):
            hots = []
            for p in range(p0, p0 + group):
                hit = hi_ref[p : p + 1, pl.ds(at, width)] == ma.astype(F32)
                loc = jnp.where(hit, lo_ref[p : p + 1, pl.ds(at, width)], -1.0).astype(BF16)
                hots.append(jnp.where(iota_b == loc, sg_ref[p : p + 1, pl.ds(at, width)].astype(BF16), zero))
            lhs = jnp.concatenate([zt_ref[p] for p in range(p0, p0 + group)], axis=1)
            acc = acc + dot(lhs, jnp.concatenate(hots, axis=0))
        for e in range(2):
            dest = 2 * d + e
            rs_ref[dest] = acc[:, e * ra : (e + 1) * ra].astype(BF16)

            @pl.when(dest != ma)
            def _():
                r_copy(dest).start()
        return carry

    lax.fori_loop(0, steps, scatter, 0)

    total = total_ref[...]
    out_t = total.T + rs_ref[ma].astype(F32)
    for k in range(1, na):
        src = peer_a(k)
        pltpu.make_async_remote_copy(
            src_ref=rs_ref.at[src], dst_ref=rr_ref.at[src], send_sem=r_send.at[src], recv_sem=r_recv.at[src],
            device_id=(src, mb), device_id_type=MESH).wait_recv()
        out_t = out_t + rr_ref[src].astype(F32)
    out_ref[...] = (out_t.T * live_a * live_b).astype(BF16)

    for k in range(1, nb):
        m_copy(k).wait_send()
        c_copy(k).wait_send()
    for k in range(1, na):
        t_copy(k, ma).wait_send()
        r_copy(peer_a(k)).wait_send()


def per_device(na, nb, amplitudes, code, counts, pair_irrep, integrals, one_body):
    ra, rb = amplitudes.shape
    pairs, ns = code.shape
    his = ns // 128
    tr = ns // (na * nb)
    dma = pltpu.SemaphoreType.DMA
    vmem = pl.BlockSpec(memory_space=pltpu.VMEM)
    return pl.pallas_call(
        functools.partial(kernel, na, nb, ns // counts.shape[0]),
        out_shape=jax.ShapeDtypeStruct((ra, rb), BF16),
        in_specs=[vmem] * 6,
        out_specs=vmem,
        scratch_shapes=[
            pltpu.VMEM((pairs, ns), F32),
            pltpu.VMEM((pairs, ns), F32),
            pltpu.VMEM((pairs, ns), F32),
            pltpu.VMEM((2 * ra, ns // 2), BF16),
            pltpu.VMEM((rb, ra), BF16),
            pltpu.VMEM((pairs, ra, rb), F32),
            pltpu.VMEM((pairs, ra, rb), F32),
            pltpu.VMEM((pairs, rb, ra), BF16),
            pltpu.VMEM((pairs * 8, pairs * 8), BF16),
            pltpu.VMEM((8, ns), F32),
            pltpu.VMEM((nb, ra, rb), BF16),
            pltpu.VMEM((na, his, tr, 128), BF16),
            pltpu.VMEM((nb, na, tr, 128), BF16),
            pltpu.VMEM((na, rb, ra), BF16),
            pltpu.VMEM((na, rb, ra), BF16),
            dma((nb,)), dma((nb,)), dma((na,)), dma((na,)),
            dma((nb,)), dma((nb,)), dma((na,)), dma((na,)),
        ],
        compiler_params=pltpu.CompilerParams(
            collective_id=0, has_side_effects=True, vmem_limit_bytes=56 * 1024 * 1024),
    )(amplitudes, code, counts.reshape(1, -1), pair_irrep.reshape(1, -1), integrals, one_body.reshape(1, -1))


def solution(mesh):
    placed = (P("aa", "ba"), P(), P(), P(), P(), P())
    body = functools.partial(per_device, mesh.shape["aa"], mesh.shape["ba"])
    return jax.shard_map(body, mesh=mesh, in_specs=placed, out_specs=P("aa", "ba"), check_vma=False)
```

time: 479 us -> 70.4 us (0.15)
  the two profiles are of different devices: /device:TPU:1 before, /device:TPU:49 now
where the time goes in v1:
time: 70.4 us; the launch traced here: 70.3 us
  Pallas kernels  68.8 us (98%)
  local copies, waits for them, and re-layouts  1.47 us (2%)
    pallas_call x1, Pallas kernels, per_device(): pl.pallas_call(functools.partial(kernel, na, nb, ns // counts.shape[0]),...  68.8 us
    unnamed x1, local copies, waits for them, and re-layouts  1.47 us

profile of v1, /device:TPU:49, one launch (start us, length us, event | category | flops | bytes accessed | tf_op | source)
XLA Modules:
  0.0 70.3 jit_solution(12750285863689841498)
XLA Ops:
  0.0 68.8 %shard_map.64 = bf16[128,256]{1,0:T(8,128)(2,1)} custom-call(bf16[128,256]{1,0:T(8,128)(2,1)} %amp_ref.1, s32[32,2048]{1,0:T(8,128)} %code_ref.1, s32[1,128]{1,0:T(1,128)} %bitcast.3, s32[1,32]{1,0:T(1,128)} %bitcast.4, bf16[32,32]{1,0:T(8,128)(2,1)} %integrals_ref.1, bf16[1,32]{1,0:T(2,128)(2,1)} %bitcast.5), custom_call_target="tpu_custom_call" | custom-call | tf_op jit(solution)/shard_map/pallas_call | solution.py:290
  68.8 1.5 %copy.8 = bf16[128,256]{1,0:T(8,128)(2,1)} copy(bf16[128,256]{1,0:T(8,128)(2,1)} %shard_map.64) | data formatting | bytes 131072

commit v2 on v1

--- a/solution.py
+++ b/solution.py
@@ -10,6 +10,9 @@
 F32 = jnp.float32
 BF16 = jnp.bfloat16
 MESH = pl.DeviceIdType.MESH
+GATHER = 8
+MIX = 8
+FLIP = 16
 
 
 def iota(shape, axis):
@@ -29,8 +32,8 @@
     amp_ref, code_ref, counts_ref, irrep_ref, integrals_ref, one_body_ref,
     out_ref,
     hi_ref, lo_ref, sg_ref, m2_ref, mt_ref, y_ref, z_ref, zt_ref, kron_ref, res_ref,
-    mg_ref, tb_ref, ta_ref, rs_ref, rr_ref,
-    m_send, m_recv, t_send, t_recv, c_send, c_recv, r_send, r_recv,
+    mg_ref, tb_ref, ta_ref, own_ref, xs_ref, xr_ref, rs_ref, rr_ref,
+    m_send, m_recv, t_send, t_recv, f_send, f_recv, c_send, c_recv, x_send, x_recv, r_send, r_recv,
 ):
     ra, rb = amp_ref.shape
     pairs, ns = code_ref.shape
@@ -41,32 +44,57 @@
     ma = lax.axis_index("aa")
     mb = lax.axis_index("ba")
 
-    def peer_a(k):
-        return lax.rem(ma + k, na)
+    nc = na // 2
+    chip = ma // 2
+    core = lax.rem(ma, 2)
+    sibling = chip * 2 + 1 - core
+
+    nx = nc // 2
+    ny = nb // 2
+    z_hi = lax.rem(chip, 2)
+    z_lo = lax.rem(mb, 2)
+
+    def peer_chip(k):
+        return lax.rem(chip + k, nc)
+
+    def along_x(k, opposite):
+        return lax.rem(chip // 2 + k, nx) * 2 + (1 - z_hi if opposite else z_hi)
+
+    def along_y(k, opposite):
+        return lax.rem(mb // 2 + k, ny) * 2 + (1 - z_lo if opposite else z_lo)
+
+    def same_core(c):
+        return c * 2 + core
 
     def peer_b(k):
         return lax.rem(mb + k, nb)
 
     barrier = pltpu.get_barrier_semaphore()
-    for k in range(1, na):
-        pl.semaphore_signal(barrier, inc=1, device_id=(peer_a(k), mb), device_id_type=MESH)
     for k in range(1, nb):
         pl.semaphore_signal(barrier, inc=1, device_id=(ma, peer_b(k)), device_id_type=MESH)
-    pl.semaphore_wait(barrier, na + nb - 2)
-
-    def m_copy(k):
+        pl.semaphore_signal(barrier, inc=1, device_id=(sibling, peer_b(k)), device_id_type=MESH)
+    for k in range(1, nc):
+        pl.semaphore_signal(barrier, inc=1, device_id=(same_core(peer_chip(k)), mb), device_id_type=MESH)
+    pl.semaphore_signal(barrier, inc=1, device_id=(sibling, mb), device_id_type=MESH)
+    pl.semaphore_wait(barrier, nc + 2 * (nb - 1))
+
+    def m_copy(k, block, dest):
+        return pltpu.make_async_remote_copy(
+            src_ref=mg_ref.at[block], dst_ref=mg_ref.at[block], send_sem=m_send.at[k], recv_sem=m_recv.at[block],
+            device_id=(ma, dest), device_id_type=MESH)
+
+    def m_first(k):
         return pltpu.make_async_remote_copy(
             src_ref=amp_ref, dst_ref=mg_ref.at[mb], send_sem=m_send.at[k], recv_sem=m_recv.at[mb],
-            device_id=(ma, peer_b(k)), device_id_type=MESH)
-
-    def m_arrived(k):
-        src = peer_b(k)
-        return pltpu.make_async_remote_copy(
-            src_ref=amp_ref, dst_ref=mg_ref.at[src], send_sem=m_send.at[k], recv_sem=m_recv.at[src],
-            device_id=(ma, src), device_id_type=MESH)
-
-    for k in range(1, nb):
-        m_copy(k).start()
+            device_id=(ma, along_y(k, k == 0)), device_id_type=MESH)
+
+    def m_relay(k):
+        return m_copy(ny + k, along_y(0, True), along_y(k, False))
+
+    near = [k for k in range(1, ny) if k in (1, ny - 1)]
+    far = [k for k in range(1, ny) if k not in near]
+    for k in [0] + near + far:
+        m_first(k).start()
 
     code = code_ref[...]
     target = jnp.abs(code) - 1
@@ -89,11 +117,6 @@
     irr_col = jnp.sum(jnp.where(eye, irr, 0), axis=1, keepdims=True)
     w = jnp.where(irr_col == irr, integrals_ref[...].astype(F32), 0.0).astype(BF16)
     w_t = dot_nt(eye.astype(F32).astype(BF16), w).astype(BF16)
-
-    grow = (iota((pairs * 8, pairs), 0) // 8 == iota((pairs * 8, pairs), 1)).astype(F32).astype(BF16)
-    wide = dot_nt(dot(grow, w).astype(BF16), grow)
-    same = iota((pairs * 8, pairs * 8), 0) % 8 == iota((pairs * 8, pairs * 8), 1) % 8
-    kron_ref[...] = jnp.where(same, wide, 0.0).astype(BF16)
 
     first = mb * rb + ma * tr
     base = pl.multiple_of((first // 128) * 128, 128)
@@ -139,13 +162,69 @@
         t_acc = t_acc + histogram(key_all[q : q + 1], lo_all[q : q + 1], val_all[q : q + 1])
     tb_ref[ma] = t_acc.astype(BF16).reshape(his, tr, 128)
 
-    def t_copy(k, slot):
-        return pltpu.make_async_remote_copy(
-            src_ref=tb_ref.at[slot], dst_ref=tb_ref.at[slot], send_sem=t_send.at[k], recv_sem=t_recv.at[slot],
-            device_id=(peer_a(k), mb), device_id_type=MESH)
-
-    for k in range(1, na):
-        t_copy(k, ma).start()
+    def t_copy(k, c, dest):
+        slot = same_core(c)
+        return pltpu.make_async_remote_copy(
+            src_ref=tb_ref.at[slot], dst_ref=tb_ref.at[slot], send_sem=t_send.at[k], recv_sem=t_recv.at[c],
+            device_id=(same_core(dest), mb), device_id_type=MESH)
+
+    def t_first(k):
+        return t_copy(k, chip, along_x(k, k == 0))
+
+    def t_relay(k):
+        return t_copy(nx + k, along_x(0, True), along_x(k, False))
+
+    def f_copy(c):
+        slot = same_core(c)
+        return pltpu.make_async_remote_copy(
+            src_ref=tb_ref.at[slot], dst_ref=tb_ref.at[slot], send_sem=f_send.at[c], recv_sem=f_recv.at[c],
+            device_id=(sibling, mb), device_id_type=MESH)
+
+    def f_arrived(c):
+        slot = c * 2 + 1 - core
+        return pltpu.make_async_remote_copy(
+            src_ref=tb_ref.at[slot], dst_ref=tb_ref.at[slot], send_sem=f_send.at[c], recv_sem=f_recv.at[c],
+            device_id=(sibling, mb), device_id_type=MESH)
+
+    def pass_on(c):
+        for k in range(1, nb):
+            for e in range(2):
+                pltpu.make_async_remote_copy(
+                    src_ref=tb_ref.at[same_core(c), chip * 2 + e], dst_ref=ta_ref.at[mb, core, c],
+                    send_sem=c_send.at[k, e], recv_sem=c_recv.at[mb, core],
+                    device_id=(chip * 2 + e, peer_b(k)), device_id_type=MESH).start()
+
+    def c_sent(k, e):
+        return pltpu.make_async_remote_copy(
+            src_ref=ta_ref.at[mb, core], dst_ref=ta_ref.at[mb, core], send_sem=c_send.at[k, e],
+            recv_sem=c_recv.at[mb, core], device_id=(chip * 2 + e, peer_b(k)), device_id_type=MESH)
+
+    def c_arrived(k, e):
+        src = peer_b(k)
+        return pltpu.make_async_remote_copy(
+            src_ref=ta_ref.at[src, e], dst_ref=ta_ref.at[src, e], send_sem=c_send.at[k, e],
+            recv_sem=c_recv.at[src, e], device_id=(chip * 2 + e, src), device_id_type=MESH)
+
+    def hand_over(c):
+        t_copy(0, c, chip).wait_recv()
+        f_copy(c).start()
+        pass_on(c)
+
+    near_x = [k for k in range(1, nx) if k in (1, nx - 1)]
+    far_x = [k for k in range(1, nx) if k not in near_x]
+    for k in [0] + near_x + far_x:
+        t_first(k).start()
+    f_copy(chip).start()
+    pass_on(chip)
+
+    m_copy(0, along_y(0, True), mb).wait_recv()
+    for k in near + far:
+        m_relay(k).start()
+
+    grow = (iota((pairs * 8, pairs), 0) // 8 == iota((pairs * 8, pairs), 1)).astype(F32).astype(BF16)
+    wide = dot_nt(dot(grow, w).astype(BF16), grow)
+    same = iota((pairs * 8, pairs * 8), 0) % 8 == iota((pairs * 8, pairs * 8), 1) % 8
+    kron_ref[...] = jnp.where(same, wide, 0.0).astype(BF16)
 
     low_a = ma * ra
     block_of = (iota((ra, blocks), 0) + low_a) // capacity
@@ -153,8 +232,14 @@
         jnp.where(block_of == iota((ra, blocks), 1), counts_ref[...].astype(F32), 0.0), axis=1, keepdims=True)
     live_a = jnp.where(((iota((ra, 1), 0) + low_a) % capacity).astype(F32) < count_a, 1.0, 0.0)
     mg_ref[mb] = amp_ref[...]
-    for k in range(1, nb):
-        m_arrived(k).wait_recv()
+    t_copy(0, along_x(0, True), chip).wait_recv()
+    for k in near_x + far_x:
+        t_relay(k).start()
+    f_copy(along_x(0, True)).start()
+    pass_on(along_x(0, True))
+    for k in range(1, ny):
+        m_copy(0, along_y(k, False), mb).wait_recv()
+        m_copy(0, along_y(k, True), mb).wait_recv()
     for j in range(nb):
         part = mg_ref[j].astype(F32) * live_a * live[:, j * rb : (j + 1) * rb]
         h = (j * rb) // (half * 128)
@@ -168,7 +253,7 @@
 
     iota_b = iota((128, rb), 0).astype(F32).astype(BF16)
 
-    def gather(q, carry):
+    def gather_one(q):
         hi_q = hi_ref[pl.ds(q, 1), pl.ds(low_b, rb)]
         lo_q = lo_ref[pl.ds(q, 1), pl.ds(low_b, rb)]
         sg_q = sg_ref[pl.ds(q, 1), pl.ds(low_b, rb)]
@@ -181,41 +266,48 @@
         got_q = dot(m2_ref[...], jnp.concatenate(hots, axis=0))
         picked = jnp.where(jnp.broadcast_to(upper, (ra, rb)), got_q[ra:], got_q[:ra])
         y_ref[q] = picked * (sg_q * live_b)
+
+    def gather(i, carry):
+        for e in range(GATHER):
+            gather_one(i * GATHER + e)
+        for at, chunks in enumerate(later):
+            @pl.when(i == min(at + 1, trips - 1))
+            def _():
+                for k, opposite in chunks:
+                    hand_over(along_x(k, opposite))
         return carry
 
-    lax.fori_loop(0, pairs, gather, 0)
-
-    def mix(g, carry):
-        at = pl.multiple_of(g * 8, 8)
-        rows = y_ref[:, pl.ds(at, 8), :].reshape(pairs * 8, rb).astype(BF16)
-        z_ref[:, pl.ds(at, 8), :] = dot(kron_ref[...], rows).reshape(pairs, 8, rb)
+    trips = pairs // GATHER
+    later = (
+        [(k, False) for k in near_x],
+        [(k, False) for k in far_x] + [(k, True) for k in near_x],
+        [(k, True) for k in far_x],
+    )
+
+    lax.fori_loop(0, pairs // GATHER, gather, 0)
+
+    def mix(i, carry):
+        for e in range(MIX):
+            at = pl.multiple_of((i * MIX + e) * 8, 8)
+            rows = y_ref[:, pl.ds(at, 8), :].reshape(pairs * 8, rb).astype(BF16)
+            z_ref[:, pl.ds(at, 8), :] = dot(kron_ref[...], rows).reshape(pairs, 8, rb)
         return carry
 
-    lax.fori_loop(0, ra // 8, mix, 0)
-
-    def flip(p, carry):
-        zt_ref[p] = z_ref[p].T.astype(BF16)
+    lax.fori_loop(0, ra // 8 // MIX, mix, 0)
+
+    def flip(i, carry):
+        for e in range(FLIP):
+            p = i * FLIP + e
+            zt_ref[p] = z_ref[p].astype(BF16).T
         return carry
 
-    lax.fori_loop(0, pairs, flip, 0)
-
-    for k in range(1, na):
-        t_copy(k, peer_a(k)).wait_recv()
-    ta_ref[mb] = tb_ref[:, ma]
-
-    def c_copy(k):
-        return pltpu.make_async_remote_copy(
-            src_ref=tb_ref.at[:, ma], dst_ref=ta_ref.at[mb], send_sem=c_send.at[k], recv_sem=c_recv.at[mb],
-            device_id=(ma, peer_b(k)), device_id_type=MESH)
-
-    def c_arrived(k):
-        src = peer_b(k)
-        return pltpu.make_async_remote_copy(
-            src_ref=tb_ref.at[:, ma], dst_ref=ta_ref.at[src], send_sem=c_send.at[k], recv_sem=c_recv.at[src],
-            device_id=(ma, src), device_id_type=MESH)
-
-    for k in range(1, nb):
-        c_copy(k).start()
+    lax.fori_loop(0, pairs // FLIP, flip, 0)
+
+    for c in range(nc):
+        f_arrived(c).wait_recv()
+    for e in range(2):
+        for c in range(nc):
+            ta_ref[mb, e, c] = tb_ref[c * 2 + e, ma]
 
     res = jnp.zeros((rb, ra), F32)
     for h in range(0, his, 2):
@@ -227,22 +319,32 @@
     total_ref[:, :] = res.T
 
     for k in range(1, nb):
-        c_arrived(k).wait_recv()
+        for e in range(2):
+            c_arrived(k, e).wait_recv()
 
     width = 2 * ra
-    steps = na // 2
     group = min(pairs, 8)
-    rows_t = width // (na * tr) if width >= na * tr else 0
-
-    def r_copy(dest):
-        return pltpu.make_async_remote_copy(
-            src_ref=rs_ref.at[dest], dst_ref=rr_ref.at[ma], send_sem=r_send.at[dest], recv_sem=r_recv.at[ma],
-            device_id=(dest, mb), device_id_type=MESH)
+
+    def x_copy(c):
+        return pltpu.make_async_remote_copy(
+            src_ref=xs_ref.at[c], dst_ref=xr_ref.at[c], send_sem=x_send.at[c], recv_sem=x_recv.at[c],
+            device_id=(sibling, mb), device_id_type=MESH)
+
+    def r_copy(c):
+        return pltpu.make_async_remote_copy(
+            src_ref=rs_ref.at[c], dst_ref=rr_ref.at[chip], send_sem=r_send.at[c], recv_sem=r_recv.at[chip],
+            device_id=(same_core(c), mb), device_id_type=MESH)
+
+    def r_arrived(c):
+        return pltpu.make_async_remote_copy(
+            src_ref=rs_ref.at[c], dst_ref=rr_ref.at[c], send_sem=r_send.at[c], recv_sem=r_recv.at[c],
+            device_id=(same_core(c), mb), device_id_type=MESH)
 
     def scatter(i, carry):
-        d = lax.rem(ma // 2 + 1 + i, steps)
+        d = peer_chip(1 + i)
         at = pl.multiple_of(d * width, 128)
-        acc = dot_nt(mt_ref[...], ta_ref[d].reshape(width, 128))
+        columns = jnp.concatenate([ta_ref[d, e, c] for c in range(nc) for e in range(2)], axis=0)
+        acc = dot_nt(mt_ref[...], columns)
         for p0 in range(0, pairs, group):
             hots = []
             for p in range(p0, p0 + group):
@@ -251,33 +353,47 @@
                 hots.append(jnp.where(iota_b == loc, sg_ref[p : p + 1, pl.ds(at, width)].astype(BF16), zero))
             lhs = jnp.concatenate([zt_ref[p] for p in range(p0, p0 + group)], axis=1)
             acc = acc + dot(lhs, jnp.concatenate(hots, axis=0))
+        first_core = core == 0
+        own_ref[d] = jnp.where(first_core, acc[:, :ra], acc[:, ra:])
+        xs_ref[d] = jnp.where(first_core, acc[:, ra:], acc[:, :ra])
+        x_copy(d).start()
+
+        @pl.when(i > 0)
+        def _():
+            send(peer_chip(i))
+        return carry
+
+    def send(d):
+        x_copy(d).wait_recv()
+        rs_ref[d] = (own_ref[d] + xr_ref[d]).astype(BF16)
+        r_copy(d).start()
+
+    lax.fori_loop(0, nc, scatter, 0)
+
+    x_copy(chip).wait_recv()
+    out_t = total_ref[...].T + own_ref[chip] + xr_ref[chip]
+    for k in range(1, nc):
+        c = peer_chip(nc - k)
+        r_arrived(c).wait_recv()
+        out_t = out_t + rr_ref[c].astype(F32)
+    out_ref[...] = (out_t.T * live_a * live_b).astype(BF16)
+
+    for k in range(ny):
+        m_first(k).wait_send()
+    for k in range(1, ny):
+        m_relay(k).wait_send()
+    for k in range(nx):
+        t_first(k).wait_send()
+    for k in range(1, nx):
+        t_relay(k).wait_send()
+    for k in range(1, nb):
         for e in range(2):
-            dest = 2 * d + e
-            rs_ref[dest] = acc[:, e * ra : (e + 1) * ra].astype(BF16)
-
-            @pl.when(dest != ma)
-            def _():
-                r_copy(dest).start()
-        return carry
-
-    lax.fori_loop(0, steps, scatter, 0)
-
-    total = total_ref[...]
-    out_t = total.T + rs_ref[ma].astype(F32)
-    for k in range(1, na):
-        src = peer_a(k)
-        pltpu.make_async_remote_copy(
-            src_ref=rs_ref.at[src], dst_ref=rr_ref.at[src], send_sem=r_send.at[src], recv_sem=r_recv.at[src],
-            device_id=(src, mb), device_id_type=MESH).wait_recv()
-        out_t = out_t + rr_ref[src].astype(F32)
-    out_ref[...] = (out_t.T * live_a * live_b).astype(BF16)
-
-    for k in range(1, nb):
-        m_copy(k).wait_send()
-        c_copy(k).wait_send()
-    for k in range(1, na):
-        t_copy(k, ma).wait_send()
-        r_copy(peer_a(k)).wait_send()
+            c_sent(k, e).wait_send()
+    for c in range(nc):
+        f_copy(c).wait_send()
+        x_copy(c).wait_send()
+    for k in range(1, nc):
+        r_copy(peer_chip(k)).wait_send()
 
 
 def per_device(na, nb, amplitudes, code, counts, pair_irrep, integrals, one_body):
@@ -305,11 +421,14 @@
             pltpu.VMEM((8, ns), F32),
             pltpu.VMEM((nb, ra, rb), BF16),
             pltpu.VMEM((na, his, tr, 128), BF16),
-            pltpu.VMEM((nb, na, tr, 128), BF16),
-            pltpu.VMEM((na, rb, ra), BF16),
-            pltpu.VMEM((na, rb, ra), BF16),
-            dma((nb,)), dma((nb,)), dma((na,)), dma((na,)),
-            dma((nb,)), dma((nb,)), dma((na,)), dma((na,)),
+            pltpu.VMEM((nb, 2, na // 2, tr, 128), BF16),
+            pltpu.VMEM((na // 2, rb, ra), F32),
+            pltpu.VMEM((na // 2, rb, ra), F32),
+            pltpu.VMEM((na // 2, rb, ra), F32),
+            pltpu.VMEM((na // 2, rb, ra), BF16),
+            pltpu.VMEM((na // 2, rb, ra), BF16),
+            dma((nb,)), dma((nb,)), dma((na // 2,)), dma((na // 2,)), dma((na // 2,)), dma((na // 2,)),
+            dma((nb, 2)), dma((nb, 2)), dma((na // 2,)), dma((na // 2,)), dma((na // 2,)), dma((na // 2,)),
         ],
         compiler_params=pltpu.CompilerParams(
             collective_id=0, has_side_effects=True, vmem_limit_bytes=56 * 1024 * 1024),

time: 70.4 us -> 45.1 us (0.64)
  the two profiles are of different devices: /device:TPU:49 before, /device:TPU:1 now
where the time goes in v2:
time: 45.1 us; the launch traced here: 45 us
  Pallas kernels  43.5 us (96%)
  local copies, waits for them, and re-layouts  1.47 us (3%)
    pallas_call x1, Pallas kernels, per_device(): pl.pallas_call(functools.partial(kernel, na, nb, ns // counts.shape[0]),...  43.5 us
    unnamed x1, local copies, waits for them, and re-layouts  1.47 us

profile of v2, /device:TPU:1, one launch (start us, length us, event | category | flops | bytes accessed | tf_op | source)
XLA Modules:
  0.0 45.0 jit_solution(4232654217049961651)
XLA Ops:
  0.0 43.5 %shard_map.64 = bf16[128,256]{1,0:T(8,128)(2,1)} custom-call(bf16[128,256]{1,0:T(8,128)(2,1)} %amp_ref.1, s32[32,2048]{1,0:T(8,128)} %code_ref.1, s32[1,128]{1,0:T(1,128)} %bitcast.3, s32[1,32]{1,0:T(1,128)} %bitcast.4, bf16[32,32]{1,0:T(8,128)(2,1)} %integrals_ref.1, bf16[1,32]{1,0:T(2,128)(2,1)} %bitcast.5), custom_call_target="tpu_custom_call" | custom-call | tf_op jit(solution)/shard_map/pallas_call | solution.py:406
  43.5 1.5 %copy.8 = bf16[128,256]{1,0:T(8,128)(2,1)} copy(bf16[128,256]{1,0:T(8,128)(2,1)} %shard_map.64) | data formatting | bytes 131072

commit v3 on v2

--- a/solution.py
+++ b/solution.py
@@ -31,9 +31,9 @@
     na, nb, capacity,
     amp_ref, code_ref, counts_ref, irrep_ref, integrals_ref, one_body_ref,
     out_ref,
-    hi_ref, lo_ref, sg_ref, m2_ref, mt_ref, y_ref, z_ref, zt_ref, kron_ref, res_ref,
+    hi_ref, lo_ref, sg_ref, kk_ref, m2_ref, mt_ref, y_ref, z_ref, zt_ref, kron_ref, live_ref,
     mg_ref, tb_ref, ta_ref, own_ref, xs_ref, xr_ref, rs_ref, rr_ref,
-    m_send, m_recv, t_send, t_recv, f_send, f_recv, c_send, c_recv, x_send, x_recv, r_send, r_recv,
+    m_send, m_recv, t_send, t_recv, f_send, f_recv, g_send, g_recv, c_send, c_recv, x_send, x_recv, r_send, r_recv,
 ):
     ra, rb = amp_ref.shape
     pairs, ns = code_ref.shape
@@ -111,6 +111,7 @@
     slots = (iota((8, ns), 1) % capacity).astype(F32)
     live8 = jnp.where(slots < dot(counts, spread), 1.0, 0.0)
     live = live8[0:1]
+    live_ref[...] = live8
 
     irr = jnp.broadcast_to(irrep_ref[...], (pairs, pairs))
     eye = iota((pairs, pairs), 0) == iota((pairs, pairs), 1)
@@ -186,24 +187,19 @@
             src_ref=tb_ref.at[slot], dst_ref=tb_ref.at[slot], send_sem=f_send.at[c], recv_sem=f_recv.at[c],
             device_id=(sibling, mb), device_id_type=MESH)
 
+    hc = nc // 2
+
     def pass_on(c):
         for k in range(1, nb):
-            for e in range(2):
-                pltpu.make_async_remote_copy(
-                    src_ref=tb_ref.at[same_core(c), chip * 2 + e], dst_ref=ta_ref.at[mb, core, c],
-                    send_sem=c_send.at[k, e], recv_sem=c_recv.at[mb, core],
-                    device_id=(chip * 2 + e, peer_b(k)), device_id_type=MESH).start()
-
-    def c_sent(k, e):
-        return pltpu.make_async_remote_copy(
-            src_ref=ta_ref.at[mb, core], dst_ref=ta_ref.at[mb, core], send_sem=c_send.at[k, e],
-            recv_sem=c_recv.at[mb, core], device_id=(chip * 2 + e, peer_b(k)), device_id_type=MESH)
-
-    def c_arrived(k, e):
-        src = peer_b(k)
+            pltpu.make_async_remote_copy(
+                src_ref=tb_ref.at[same_core(c), pl.ds(chip * 2, 2)], dst_ref=ta_ref.at[mb, core, lax.rem(c, hc)],
+                send_sem=c_send.at[k, c // hc], recv_sem=c_recv.at[mb, core],
+                device_id=(chip * 2 + c // hc, peer_b(k)), device_id_type=MESH).start()
+
+    def c_copy(k, src, e):
         return pltpu.make_async_remote_copy(
             src_ref=ta_ref.at[src, e], dst_ref=ta_ref.at[src, e], send_sem=c_send.at[k, e],
-            recv_sem=c_recv.at[src, e], device_id=(chip * 2 + e, src), device_id_type=MESH)
+            recv_sem=c_recv.at[src, e], device_id=(chip * 2 + e, peer_b(k)), device_id_type=MESH)
 
     def hand_over(c):
         t_copy(0, c, chip).wait_recv()
@@ -232,59 +228,84 @@
         jnp.where(block_of == iota((ra, blocks), 1), counts_ref[...].astype(F32), 0.0), axis=1, keepdims=True)
     live_a = jnp.where(((iota((ra, 1), 0) + low_a) % capacity).astype(F32) < count_a, 1.0, 0.0)
     mg_ref[mb] = amp_ref[...]
-    t_copy(0, along_x(0, True), chip).wait_recv()
-    for k in near_x + far_x:
-        t_relay(k).start()
-    f_copy(along_x(0, True)).start()
-    pass_on(along_x(0, True))
+    low_b = pl.multiple_of(mb * rb, 128)
+    live_b = live_ref[0:1, pl.ds(low_b, rb)]
+    mine_f = amp_ref[...].astype(F32) * live_a * live_b
+    mt_ref[core] = mine_f.T.astype(BF16)
+    g_copy = pltpu.make_async_remote_copy(
+        src_ref=mt_ref.at[core], dst_ref=mt_ref.at[core], send_sem=g_send, recv_sem=g_recv,
+        device_id=(sibling, mb), device_id_type=MESH)
+    g_copy.start()
+
+    hi_b = hi_ref[:, pl.ds(low_b, rb)]
+    y_b = jnp.floor(hi_b * 0.25)
+    rest_b = hi_b - 4.0 * y_b
+    for turn in range(2):
+        e_b = rest_b - 2.0 * (1 - z_lo if turn else z_lo).astype(F32)
+        inside = (e_b >= 0.0) & (e_b < 2.0)
+        kk_ref[turn] = jnp.where(inside, 2.0 * y_b + e_b, -1.0)
+
+    iota_b = iota((128, rb), 0).astype(F32).astype(BF16)
+
+    def arrange(turn):
+        for y in range(ny):
+            block = 2 * y + (1 - z_lo if turn else z_lo)
+            on = live_ref[0:1, pl.ds(pl.multiple_of(block * rb, 128), rb)]
+            part = (mg_ref[block].astype(F32) * live_a * on).astype(BF16)
+            for e in range(2):
+                u = 2 * y + e
+                h, at = u // ny, (u % ny) * 128
+                m2_ref[turn, h * ra : (h + 1) * ra, at : at + 128] = part[:, e * 128 : (e + 1) * 128]
+
+    def gather_one(turn, q):
+        kk_q = kk_ref[turn, pl.ds(q, 1), :]
+        lo_q = lo_ref[pl.ds(q, 1), pl.ds(low_b, rb)]
+        sg_q = sg_ref[pl.ds(q, 1), pl.ds(low_b, rb)]
+        upper = kk_q >= float(ny)
+        inner = jnp.where(upper, kk_q - float(ny), kk_q)
+        hots = []
+        for j in range(ny):
+            loc = jnp.where(inner == float(j), lo_q, -1.0).astype(BF16)
+            hots.append(jnp.where(iota_b == loc, one, zero))
+        got_q = dot(m2_ref[turn], jnp.concatenate(hots, axis=0))
+        picked = jnp.where(jnp.broadcast_to(upper, (ra, rb)), got_q[ra:], got_q[:ra]) * (sg_q * live_b)
+        y_ref[q] = y_ref[q] + picked if turn else picked
+
+    trips = pairs // GATHER
+
     for k in range(1, ny):
         m_copy(0, along_y(k, False), mb).wait_recv()
+    arrange(0)
+
+    def gather_own(i, carry):
+        for e in range(GATHER):
+            gather_one(0, i * GATHER + e)
+
+        @pl.when(i == trips - 2)
+        def _():
+            t_copy(0, along_x(0, True), chip).wait_recv()
+            for k in near_x + far_x:
+                t_relay(k).start()
+            f_copy(along_x(0, True)).start()
+            pass_on(along_x(0, True))
+        return carry
+
+    lax.fori_loop(0, trips, gather_own, 0)
+    for k in near_x + far_x:
+        hand_over(along_x(k, False))
+    for k in range(1, ny):
         m_copy(0, along_y(k, True), mb).wait_recv()
-    for j in range(nb):
-        part = mg_ref[j].astype(F32) * live_a * live[:, j * rb : (j + 1) * rb]
-        h = (j * rb) // (half * 128)
-        at = j * rb - h * half * 128
-        m2_ref[h * ra : (h + 1) * ra, at : at + rb] = part.astype(BF16)
-    low_b = pl.multiple_of(mb * rb, 128)
-    res_ref[...] = live8
-    live_b = res_ref[0:1, pl.ds(low_b, rb)]
-    mine_f = amp_ref[...].astype(F32) * live_a * live_b
-    mt_ref[...] = mine_f.T.astype(BF16)
-
-    iota_b = iota((128, rb), 0).astype(F32).astype(BF16)
-
-    def gather_one(q):
-        hi_q = hi_ref[pl.ds(q, 1), pl.ds(low_b, rb)]
-        lo_q = lo_ref[pl.ds(q, 1), pl.ds(low_b, rb)]
-        sg_q = sg_ref[pl.ds(q, 1), pl.ds(low_b, rb)]
-        upper = hi_q >= float(half)
-        hi_in = jnp.where(upper, hi_q - float(half), hi_q)
-        hots = []
-        for j in range(half):
-            loc = jnp.where(hi_in == float(j), lo_q, -1.0).astype(BF16)
-            hots.append(jnp.where(iota_b == loc, one, zero))
-        got_q = dot(m2_ref[...], jnp.concatenate(hots, axis=0))
-        picked = jnp.where(jnp.broadcast_to(upper, (ra, rb)), got_q[ra:], got_q[:ra])
-        y_ref[q] = picked * (sg_q * live_b)
-
-    def gather(i, carry):
+    arrange(1)
+
+    def gather_other(i, carry):
         for e in range(GATHER):
-            gather_one(i * GATHER + e)
-        for at, chunks in enumerate(later):
-            @pl.when(i == min(at + 1, trips - 1))
-            def _():
-                for k, opposite in chunks:
-                    hand_over(along_x(k, opposite))
+            gather_one(1, i * GATHER + e)
+
         return carry
 
-    trips = pairs // GATHER
-    later = (
-        [(k, False) for k in near_x],
-        [(k, False) for k in far_x] + [(k, True) for k in near_x],
-        [(k, True) for k in far_x],
-    )
-
-    lax.fori_loop(0, pairs // GATHER, gather, 0)
+    lax.fori_loop(0, trips, gather_other, 0)
+    for k in near_x:
+        hand_over(along_x(k, True))
 
     def mix(i, carry):
         for e in range(MIX):
@@ -294,6 +315,8 @@
         return carry
 
     lax.fori_loop(0, ra // 8 // MIX, mix, 0)
+    for k in far_x:
+        hand_over(along_x(k, True))
 
     def flip(i, carry):
         for e in range(FLIP):
@@ -306,21 +329,22 @@
     for c in range(nc):
         f_arrived(c).wait_recv()
     for e in range(2):
-        for c in range(nc):
-            ta_ref[mb, e, c] = tb_ref[c * 2 + e, ma]
+        for c in range(hc):
+            ta_ref[mb, e, c] = tb_ref[core * nc + 2 * c + e, pl.ds(chip * 2, 2)]
 
     res = jnp.zeros((rb, ra), F32)
-    for h in range(0, his, 2):
-        lhs = jnp.concatenate([tb_ref[:, h].reshape(rb, 128), tb_ref[:, h + 1].reshape(rb, 128)], axis=1)
-        part = h // half
-        at = (h - part * half) * 128
-        res = res + dot_nt(lhs, m2_ref[part * ra : (part + 1) * ra, at : at + 256])
+    for turn in range(2):
+        for u in range(0, 2 * ny, min(ny, 2)):
+            parts = []
+            for v in range(u, u + min(ny, 2)):
+                h = 4 * (v // 2) + 2 * (1 - z_lo if turn else z_lo) + v % 2
+                parts.append(tb_ref[:, h].reshape(rb, 128))
+            h, at = u // ny, (u % ny) * 128
+            res = res + dot_nt(
+                jnp.concatenate(parts, axis=1), m2_ref[turn, h * ra : (h + 1) * ra, at : at + 128 * len(parts)])
     total_ref = z_ref.at[0]
     total_ref[:, :] = res.T
-
-    for k in range(1, nb):
-        for e in range(2):
-            c_arrived(k, e).wait_recv()
+    g_copy.wait()
 
     width = 2 * ra
     group = min(pairs, 8)
@@ -341,10 +365,9 @@
             device_id=(same_core(c), mb), device_id_type=MESH)
 
     def scatter(i, carry):
-        d = peer_chip(1 + i)
+        d = turn_of(i)
         at = pl.multiple_of(d * width, 128)
-        columns = jnp.concatenate([ta_ref[d, e, c] for c in range(nc) for e in range(2)], axis=0)
-        acc = dot_nt(mt_ref[...], columns)
+        acc = jnp.zeros((rb, width), F32)
         for p0 in range(0, pairs, group):
             hots = []
             for p in range(p0, p0 + group):
@@ -360,20 +383,36 @@
 
         @pl.when(i > 0)
         def _():
-            send(peer_chip(i))
+            send(turn_of(i - 1))
         return carry
 
+    def turn_of(i):
+        return lax.rem(chip // 2 + nx - 1 - lax.rem(i, nx), nx) * 2 + jnp.where(i < nx, 1 - z_hi, z_hi)
+
+    def arrival(i):
+        return lax.rem(chip // 2 + 1 + i % nx, nx) * 2 + (1 - z_hi if i < nx else z_hi)
+
+    def summed(d):
+        @pl.when(d != mb)
+        def _():
+            for e in range(2):
+                c_copy(1, d, e).wait_recv()
+        x_copy(d).wait_recv()
+        acc = own_ref[d] + xr_ref[d]
+        for h in range(2):
+            rows = jnp.concatenate([ta_ref[d, e, c, h] for c in range(hc) for e in range(2)], axis=0)
+            acc = acc + dot_nt(mt_ref[h], rows)
+        return acc
+
     def send(d):
-        x_copy(d).wait_recv()
-        rs_ref[d] = (own_ref[d] + xr_ref[d]).astype(BF16)
+        rs_ref[d] = summed(d).astype(BF16)
         r_copy(d).start()
 
     lax.fori_loop(0, nc, scatter, 0)
 
-    x_copy(chip).wait_recv()
-    out_t = total_ref[...].T + own_ref[chip] + xr_ref[chip]
-    for k in range(1, nc):
-        c = peer_chip(nc - k)
+    out_t = total_ref[...].T + summed(chip)
+    for i in range(nc - 1):
+        c = arrival(i)
         r_arrived(c).wait_recv()
         out_t = out_t + rr_ref[c].astype(F32)
     out_ref[...] = (out_t.T * live_a * live_b).astype(BF16)
@@ -388,7 +427,7 @@
         t_relay(k).wait_send()
     for k in range(1, nb):
         for e in range(2):
-            c_sent(k, e).wait_send()
+            c_copy(k, mb, e).wait_send()
     for c in range(nc):
         f_copy(c).wait_send()
         x_copy(c).wait_send()
@@ -412,8 +451,9 @@
             pltpu.VMEM((pairs, ns), F32),
             pltpu.VMEM((pairs, ns), F32),
             pltpu.VMEM((pairs, ns), F32),
-            pltpu.VMEM((2 * ra, ns // 2), BF16),
-            pltpu.VMEM((rb, ra), BF16),
+            pltpu.VMEM((2, pairs, rb), F32),
+            pltpu.VMEM((2, 2 * ra, ns // 4), BF16),
+            pltpu.VMEM((2, rb, ra), BF16),
             pltpu.VMEM((pairs, ra, rb), F32),
             pltpu.VMEM((pairs, ra, rb), F32),
             pltpu.VMEM((pairs, rb, ra), BF16),
@@ -421,13 +461,13 @@
             pltpu.VMEM((8, ns), F32),
             pltpu.VMEM((nb, ra, rb), BF16),
             pltpu.VMEM((na, his, tr, 128), BF16),
-            pltpu.VMEM((nb, 2, na // 2, tr, 128), BF16),
+            pltpu.VMEM((nb, 2, na // 4, 2, tr, 128), BF16),
             pltpu.VMEM((na // 2, rb, ra), F32),
             pltpu.VMEM((na // 2, rb, ra), F32),
             pltpu.VMEM((na // 2, rb, ra), F32),
             pltpu.VMEM((na // 2, rb, ra), BF16),
             pltpu.VMEM((na // 2, rb, ra), BF16),
-            dma((nb,)), dma((nb,)), dma((na // 2,)), dma((na // 2,)), dma((na // 2,)), dma((na // 2,)),
+            dma((nb,)), dma((nb,)), dma((na // 2,)), dma((na // 2,)), dma((na // 2,)), dma((na // 2,)), dma, dma,
             dma((nb, 2)), dma((nb, 2)), dma((na // 2,)), dma((na // 2,)), dma((na // 2,)), dma((na // 2,)),
         ],
         compiler_params=pltpu.CompilerParams(

time: 45.1 us -> 40.1 us (0.89)
  Pallas kernels: 43.5 us -> 38.5 us
    pallas_call x1, Pallas kernels: 43.5 us -> 38.5 us  [per_device(): pl.pallas_call(functools.partial(kernel, na, nb, ns // counts.shape[0]),...]
where the time goes in v3:
time: 40.1 us; the launch traced here: 39.9 us
  Pallas kernels  38.5 us (96%)
  local copies, waits for them, and re-layouts  1.47 us (4%)
    pallas_call x1, Pallas kernels, per_device(): pl.pallas_call(functools.partial(kernel, na, nb, ns // counts.shape[0]),...  38.5 us
    unnamed x1, local copies, waits for them, and re-layouts  1.47 us

profile of v3, /device:TPU:1, one launch (start us, length us, event | category | flops | bytes accessed | tf_op | source)
XLA Modules:
  0.0 39.9 jit_solution(15190218388480556078)
XLA Ops:
  0.0 38.5 %shard_map.64 = bf16[128,256]{1,0:T(8,128)(2,1)} custom-call(bf16[128,256]{1,0:T(8,128)(2,1)} %amp_ref.1, s32[32,2048]{1,0:T(8,128)} %code_ref.1, s32[1,128]{1,0:T(1,128)} %bitcast.3, s32[1,32]{1,0:T(1,128)} %bitcast.4, bf16[32,32]{1,0:T(8,128)(2,1)} %integrals_ref.1, bf16[1,32]{1,0:T(2,128)(2,1)} %bitcast.5), custom_call_target="tpu_custom_call" | custom-call | tf_op jit(solution)/shard_map/pallas_call | solution.py:445
  38.5 1.5 %copy.8 = bf16[128,256]{1,0:T(8,128)(2,1)} copy(bf16[128,256]{1,0:T(8,128)(2,1)} %shard_map.64) | data formatting | bytes 131072

commit v4 on v3

--- a/solution.py
+++ b/solution.py
@@ -12,7 +12,7 @@
 MESH = pl.DeviceIdType.MESH
 GATHER = 8
 MIX = 8
-FLIP = 16
+LAG = 3
 
 
 def iota(shape, axis):
@@ -29,8 +29,9 @@
 
 def kernel(
     na, nb, capacity,
-    amp_ref, code_ref, counts_ref, irrep_ref, integrals_ref, one_body_ref,
+    amp_in, code_in, counts_in, irrep_in, integrals_in, one_body_in,
     out_ref,
+    amp_ref, code_ref, counts_ref, irrep_ref, integrals_ref, one_body_ref, in_sem,
     hi_ref, lo_ref, sg_ref, kk_ref, m2_ref, mt_ref, y_ref, z_ref, zt_ref, kron_ref, live_ref,
     mg_ref, tb_ref, ta_ref, own_ref, xs_ref, xr_ref, rs_ref, rr_ref,
     m_send, m_recv, t_send, t_recv, f_send, f_recv, g_send, g_recv, c_send, c_recv, x_send, x_recv, r_send, r_recv,
@@ -76,6 +77,15 @@
     for k in range(1, nc):
         pl.semaphore_signal(barrier, inc=1, device_id=(same_core(peer_chip(k)), mb), device_id_type=MESH)
     pl.semaphore_signal(barrier, inc=1, device_id=(sibling, mb), device_id_type=MESH)
+    loads = [
+        pltpu.make_async_copy(src, dst, in_sem.at[i])
+        for i, (src, dst) in enumerate((
+            (amp_in, amp_ref), (code_in, code_ref), (counts_in, counts_ref), (irrep_in, irrep_ref),
+            (integrals_in, integrals_ref), (one_body_in, one_body_ref)))
+    ]
+    for load in loads:
+        load.start()
+    loads[0].wait()
     pl.semaphore_wait(barrier, nc + 2 * (nb - 1))
 
     def m_copy(k, block, dest):
@@ -95,6 +105,9 @@
     far = [k for k in range(1, ny) if k not in near]
     for k in [0] + near + far:
         m_first(k).start()
+
+    for load in loads[1:]:
+        load.wait()
 
     code = code_ref[...]
     target = jnp.abs(code) - 1
@@ -148,20 +161,35 @@
             sel.append(jnp.where(iota128 == loc, one, zero))
         got = got + dot(planes[:, h * 128 : (h + 2) * 128], jnp.concatenate(sel, axis=0))
     row = (iota((pairs, n), 1) % tr).astype(F32)
-    key_all = got[0:pairs] * float(tr) + row
-    lo_all = got[pairs : 2 * pairs]
-    val_all = 0.5 * w_wide * got[2 * pairs :] * k_sg
-    iota_keys = iota((keys, n), 0).astype(F32).astype(BF16)
-
-    def histogram(key, low, val):
-        a = jnp.where(iota_keys == key.astype(BF16), val.astype(BF16), zero)
-        b = jnp.where(iota128 == low.astype(BF16), one, zero)
-        return dot_nt(a, b)
-
-    t_acc = histogram(k_hi * float(tr) + row[0:1], k_lo, o_wide * k_sg)
+
+    def split(high, low):
+        upper = jnp.floor(high * 0.5)
+        return upper * float(tr), (high - 2.0 * upper) * 128.0 + low
+
+    key_all, low_all = split(got[0:pairs], got[pairs : 2 * pairs])
+    key_all = (key_all + row).astype(BF16)
+    val_all = (0.5 * w_wide * got[2 * pairs :] * k_sg).astype(BF16)
+    key_one, low_one = split(k_hi, k_lo)
+    key_one = (key_one + row[0:1]).astype(BF16)
+    low_t = jnp.concatenate([low_all, jnp.broadcast_to(low_one, (8, n))], axis=0).T
+    low_t = low_t.astype(BF16)
+    iota_keys = iota((keys // 2, n), 0).astype(F32).astype(BF16)
+    iota_low = iota((n, 256), 1).astype(F32).astype(BF16)
+
+    def histogram(key, val, at):
+        a = jnp.where(iota_keys == key, val, zero)
+        hit = iota_low == jnp.broadcast_to(low_t[:, at : at + 1], (n, 256))
+        b = jnp.where(hit, one, zero)
+        return dot(a, b)
+
+    t_acc = histogram(key_one, (o_wide * k_sg).astype(BF16), pairs)
     for q in range(pairs):
-        t_acc = t_acc + histogram(key_all[q : q + 1], lo_all[q : q + 1], val_all[q : q + 1])
-    tb_ref[ma] = t_acc.astype(BF16).reshape(his, tr, 128)
+        t_acc = t_acc + histogram(key_all[q : q + 1], val_all[q : q + 1], q)
+    t_acc = t_acc.astype(BF16)
+    for h in range(2):
+        part = t_acc[:, h * 128 : (h + 1) * 128].reshape(his // 2, tr, 128)
+        for g in range(his // 2):
+            tb_ref[ma, 2 * g + h] = part[g]
 
     def t_copy(k, c, dest):
         slot = same_core(c)
@@ -188,6 +216,7 @@
             device_id=(sibling, mb), device_id_type=MESH)
 
     hc = nc // 2
+    lag = min(LAG, hc)
 
     def pass_on(c):
         for k in range(1, nb):
@@ -269,7 +298,10 @@
             hots.append(jnp.where(iota_b == loc, one, zero))
         got_q = dot(m2_ref[turn], jnp.concatenate(hots, axis=0))
         picked = jnp.where(jnp.broadcast_to(upper, (ra, rb)), got_q[ra:], got_q[:ra]) * (sg_q * live_b)
-        y_ref[q] = y_ref[q] + picked if turn else picked
+        if turn:
+            z_ref[q] = (y_ref[q] + picked).astype(BF16).T.astype(F32)
+        else:
+            y_ref[q] = picked
 
     trips = pairs // GATHER
 
@@ -309,42 +341,16 @@
 
     def mix(i, carry):
         for e in range(MIX):
-            at = pl.multiple_of((i * MIX + e) * 8, 8)
-            rows = y_ref[:, pl.ds(at, 8), :].reshape(pairs * 8, rb).astype(BF16)
-            z_ref[:, pl.ds(at, 8), :] = dot(kron_ref[...], rows).reshape(pairs, 8, rb)
+            at = pl.multiple_of((i * MIX + e) * 16, 16)
+            rows = [z_ref[:, pl.ds(at + 8 * h, 8), :].reshape(pairs * 8, ra) for h in range(2)]
+            mixed = dot(kron_ref[...], jnp.concatenate(rows, axis=1).astype(BF16)).reshape(pairs, 8, 2 * ra)
+            zt_ref[:, pl.ds(at, 16), :] = jnp.concatenate([mixed[:, :, :ra], mixed[:, :, ra:]], axis=1).astype(BF16)
         return carry
 
-    lax.fori_loop(0, ra // 8 // MIX, mix, 0)
+    lax.fori_loop(0, rb // 16 // MIX, mix, 0)
     for k in far_x:
         hand_over(along_x(k, True))
 
-    def flip(i, carry):
-        for e in range(FLIP):
-            p = i * FLIP + e
-            zt_ref[p] = z_ref[p].astype(BF16).T
-        return carry
-
-    lax.fori_loop(0, pairs // FLIP, flip, 0)
-
-    for c in range(nc):
-        f_arrived(c).wait_recv()
-    for e in range(2):
-        for c in range(hc):
-            ta_ref[mb, e, c] = tb_ref[core * nc + 2 * c + e, pl.ds(chip * 2, 2)]
-
-    res = jnp.zeros((rb, ra), F32)
-    for turn in range(2):
-        for u in range(0, 2 * ny, min(ny, 2)):
-            parts = []
-            for v in range(u, u + min(ny, 2)):
-                h = 4 * (v // 2) + 2 * (1 - z_lo if turn else z_lo) + v % 2
-                parts.append(tb_ref[:, h].reshape(rb, 128))
-            h, at = u // ny, (u % ny) * 128
-            res = res + dot_nt(
-                jnp.concatenate(parts, axis=1), m2_ref[turn, h * ra : (h + 1) * ra, at : at + 128 * len(parts)])
-    total_ref = z_ref.at[0]
-    total_ref[:, :] = res.T
-    g_copy.wait()
 
     width = 2 * ra
     group = min(pairs, 8)
@@ -381,9 +387,23 @@
         xs_ref[d] = jnp.where(first_core, acc[:, ra:], acc[:, :ra])
         x_copy(d).start()
 
-        @pl.when(i > 0)
+        @pl.when(i == lag - 1)
         def _():
-            send(turn_of(i - 1))
+            for c in range(nc):
+                f_arrived(c).wait_recv()
+            for e in range(2):
+                for c in range(hc):
+                    ta_ref[mb, e, c] = tb_ref[core * nc + 2 * c + e, pl.ds(chip * 2, 2)]
+            g_copy.wait()
+
+        @pl.when(i >= lag)
+        def _():
+            send(turn_of(i - lag))
+
+        @pl.when(i == nc - 1)
+        def _():
+            if lag > 1:
+                send(turn_of(nc - lag))
         return carry
 
     def turn_of(i):
@@ -409,8 +429,22 @@
         r_copy(d).start()
 
     lax.fori_loop(0, nc, scatter, 0)
-
-    out_t = total_ref[...].T + summed(chip)
+    for i in range(nc - lag + 1, nc - 1):
+        send(turn_of(i))
+
+    res = jnp.zeros((rb, ra), F32)
+    for turn in range(2):
+        for u in range(0, 2 * ny, min(ny, 2)):
+            parts = []
+            for v in range(u, u + min(ny, 2)):
+                h = 4 * (v // 2) + 2 * (1 - z_lo if turn else z_lo) + v % 2
+                parts.append(tb_ref[:, h].reshape(rb, 128))
+            h, at = u // ny, (u % ny) * 128
+            res = res + dot_nt(
+                jnp.concatenate(parts, axis=1), m2_ref[turn, h * ra : (h + 1) * ra, at : at + 128 * len(parts)])
+
+
+    out_t = res + summed(chip)
     for i in range(nc - 1):
         c = arrival(i)
         r_arrived(c).wait_recv()
@@ -445,9 +479,16 @@
     return pl.pallas_call(
         functools.partial(kernel, na, nb, ns // counts.shape[0]),
         out_shape=jax.ShapeDtypeStruct((ra, rb), BF16),
-        in_specs=[vmem] * 6,
+        in_specs=[pl.BlockSpec(memory_space=pl.ANY)] * 6,
         out_specs=vmem,
         scratch_shapes=[
+            pltpu.VMEM((ra, rb), BF16),
+            pltpu.VMEM((pairs, ns), jnp.int32),
+            pltpu.VMEM((1, counts.shape[0]), jnp.int32),
+            pltpu.VMEM((1, pairs), jnp.int32),
+            pltpu.VMEM((pairs, pairs), BF16),
+            pltpu.VMEM((1, pairs), BF16),
+            dma((6,)),
             pltpu.VMEM((pairs, ns), F32),
             pltpu.VMEM((pairs, ns), F32),
             pltpu.VMEM((pairs, ns), F32),
@@ -455,7 +496,7 @@
             pltpu.VMEM((2, 2 * ra, ns // 4), BF16),
             pltpu.VMEM((2, rb, ra), BF16),
             pltpu.VMEM((pairs, ra, rb), F32),
-            pltpu.VMEM((pairs, ra, rb), F32),
+            pltpu.VMEM((pairs, rb, ra), F32),
             pltpu.VMEM((pairs, rb, ra), BF16),
             pltpu.VMEM((pairs * 8, pairs * 8), BF16),
             pltpu.VMEM((8, ns), F32),

time: 40.1 us -> 37.8 us (0.943)
  Pallas kernels: 38.5 us -> 36.1 us
    pallas_call x1, Pallas kernels: 38.5 us -> 36.1 us  [per_device(): pl.pallas_call(functools.partial(kernel, na, nb, ns // counts.shape[0]),...]
where the time goes in v4:
time: 37.8 us; the launch traced here: 37.6 us
  Pallas kernels  36.1 us (96%)
  local copies, waits for them, and re-layouts  1.47 us (4%)
    pallas_call x1, Pallas kernels, per_device(): pl.pallas_call(functools.partial(kernel, na, nb, ns // counts.shape[0]),...  36.1 us
    unnamed x1, local copies, waits for them, and re-layouts  1.47 us

profile of v4, /device:TPU:1, one launch (start us, length us, event | category | flops | bytes accessed | tf_op | source)
XLA Modules:
  0.0 37.6 jit_solution(9416091239155359560)
XLA Ops:
  0.0 36.1 %shard_map.64 = bf16[128,256]{1,0:T(8,128)(2,1)} custom-call(bf16[128,256]{1,0:T(8,128)(2,1)} %amp_in.1, s32[32,2048]{1,0:T(8,128)} %code_in.1, s32[1,128]{1,0:T(1,128)} %bitcast.3, s32[1,32]{1,0:T(1,128)} %bitcast.4, bf16[32,32]{1,0:T(8,128)(2,1)} %integrals_in.1, bf16[1,32]{1,0:T(2,128)(2,1)} %bitcast.5), custom_call_target="tpu_custom_call" | custom-call | tf_op jit(solution)/shard_map/pallas_call | solution.py:479
  36.2 1.5 %copy.8 = bf16[128,256]{1,0:T(8,128)(2,1)} copy(bf16[128,256]{1,0:T(8,128)(2,1)} %shard_map.64) | data formatting | bytes 131072

commit v5 on v4

--- a/solution.py
+++ b/solution.py
@@ -11,7 +11,7 @@
 BF16 = jnp.bfloat16
 MESH = pl.DeviceIdType.MESH
 GATHER = 8
-MIX = 8
+MIX = 16
 LAG = 3
 
 
@@ -313,7 +313,7 @@
         for e in range(GATHER):
             gather_one(0, i * GATHER + e)
 
-        @pl.when(i == trips - 2)
+        @pl.when(i == trips - 3)
         def _():
             t_copy(0, along_x(0, True), chip).wait_recv()
             for k in near_x + far_x:
@@ -333,10 +333,14 @@
         for e in range(GATHER):
             gather_one(1, i * GATHER + e)
 
+        @pl.when(i == trips - 2)
+        def _():
+            for k in near_x:
+                hand_over(along_x(k, True))
         return carry
 
     lax.fori_loop(0, trips, gather_other, 0)
-    for k in near_x:
+    for k in far_x:
         hand_over(along_x(k, True))
 
     def mix(i, carry):
@@ -348,8 +352,6 @@
         return carry
 
     lax.fori_loop(0, rb // 16 // MIX, mix, 0)
-    for k in far_x:
-        hand_over(along_x(k, True))
 
 
     width = 2 * ra

time: 37.8 us -> 37.3 us (0.987)
  Pallas kernels: 36.1 us -> 35.6 us
    pallas_call x1, Pallas kernels: 36.1 us -> 35.6 us  [per_device(): pl.pallas_call(functools.partial(kernel, na, nb, ns // counts.shape[0]),...]
where the time goes in v5:
time: 37.3 us; the launch traced here: 37.1 us
  Pallas kernels  35.6 us (95%)
  local copies, waits for them, and re-layouts  1.47 us (4%)
    pallas_call x1, Pallas kernels, per_device(): pl.pallas_call(functools.partial(kernel, na, nb, ns // counts.shape[0]),...  35.6 us
    unnamed x1, local copies, waits for them, and re-layouts  1.47 us

profile of v5, /device:TPU:1, one launch (start us, length us, event | category | flops | bytes accessed | tf_op | source)
XLA Modules:
  0.0 37.1 jit_solution(12047838958709341387)
XLA Ops:
  0.0 35.6 %shard_map.64 = bf16[128,256]{1,0:T(8,128)(2,1)} custom-call(bf16[128,256]{1,0:T(8,128)(2,1)} %amp_in.1, s32[32,2048]{1,0:T(8,128)} %code_in.1, s32[1,128]{1,0:T(1,128)} %bitcast.3, s32[1,32]{1,0:T(1,128)} %bitcast.4, bf16[32,32]{1,0:T(8,128)(2,1)} %integrals_in.1, bf16[1,32]{1,0:T(2,128)(2,1)} %bitcast.5), custom_call_target="tpu_custom_call" | custom-call | tf_op jit(solution)/shard_map/pallas_call | solution.py:481
  35.6 1.5 %copy.8 = bf16[128,256]{1,0:T(8,128)(2,1)} copy(bf16[128,256]{1,0:T(8,128)(2,1)} %shard_map.64) | data formatting | bytes 131072

commit v6 on v5

--- a/solution.py
+++ b/solution.py
@@ -355,7 +355,7 @@
 
 
     width = 2 * ra
-    group = min(pairs, 8)
+    group = min(pairs, 4)
 
     def x_copy(c):
         return pltpu.make_async_remote_copy(

time: 37.3 us -> 37.2 us (level)
  no operation moved by 1% of the time
where the time goes in v6:
time: 37.2 us; the launch traced here: 37.1 us
  Pallas kernels  35.6 us (96%)
  local copies, waits for them, and re-layouts  1.47 us (4%)
    pallas_call x1, Pallas kernels, per_device(): pl.pallas_call(functools.partial(kernel, na, nb, ns // counts.shape[0]),...  35.6 us
    unnamed x1, local copies, waits for them, and re-layouts  1.47 us

profile of v6, /device:TPU:1, one launch (start us, length us, event | category | flops | bytes accessed | tf_op | source)
XLA Modules:
  0.0 37.1 jit_solution(17909454768940511746)
XLA Ops:
  0.0 35.6 %shard_map.64 = bf16[128,256]{1,0:T(8,128)(2,1)} custom-call(bf16[128,256]{1,0:T(8,128)(2,1)} %amp_in.1, s32[32,2048]{1,0:T(8,128)} %code_in.1, s32[1,128]{1,0:T(1,128)} %bitcast.3, s32[1,32]{1,0:T(1,128)} %bitcast.4, bf16[32,32]{1,0:T(8,128)(2,1)} %integrals_in.1, bf16[1,32]{1,0:T(2,128)(2,1)} %bitcast.5), custom_call_target="tpu_custom_call" | custom-call | tf_op jit(solution)/shard_map/pallas_call | solution.py:481
  35.6 1.5 %copy.8 = bf16[128,256]{1,0:T(8,128)(2,1)} copy(bf16[128,256]{1,0:T(8,128)(2,1)} %shard_map.64) | data formatting | bytes 131072
